TPU v7x, 32 devices: a whole 2x2x4 slice. The times are simulated.
32 devices in a mesh: groups: 2 (over y), ep: 4 (over x, core), tp: 4 (over z).
Axes of the slice: x: 2, y: 2, z: 4, core: 2. Of those that a mesh axis runs over, the one named last changes fastest.
Arguments:
- tokens: bfloat16 [256, 7168], P(('groups', 'ep')), parts along dimension 0, may hold values from -6 to 6
- w_gate: bfloat16 [16, 7168, 2048], P('ep', None, 'tp'), may hold values from -0.0625 to 0.0625
- w_up: bfloat16 [16, 7168, 2048], P('ep', None, 'tp'), may hold values from -0.0625 to 0.0625
- w_down: bfloat16 [16, 2048, 7168], P('ep', 'tp'), may hold values from -0.1875 to 0.1875
- router_logits: float32 [256, 8], P(('groups', 'ep')), parts along dimension 0, may hold values from -6 to 6
- expert_ids: int32 [256, 8], P(('groups', 'ep')), parts along dimension 0, may hold values from 0 to 15, all different within a row; in each aligned block of 32 rows (0 to 31, 32 to 63, ...) at most 24 rows name the same one
- draft_lengths: int32 [32], P(('groups', 'ep')), parts along dimension 0, may hold values from 7 to 8
- accept_mask: int32 [32, 8], P(('groups', 'ep')), parts along dimension 0, may hold values 0 or 1
Outputs:
- mixed: bfloat16 [256, 7168], P(('groups', 'ep'), 'tp'), parts along dimension 0
- accepted: int32 [2], P('groups'), parts along dimension 0
There are 2 independent parts, one for each index of `groups`. A program takes and returns all parts, laid end to end along the dimension named above; an argument that names none is the same for every part. Nothing has to cross between parts.
Inputs may be any that keep to these rules, and one draw needn't show every extreme that they name: `expert_ids`: each row names 8 different experts. Among the rows of one ep index (aligned blocks of 32 rows) no expert is named by more than 24 rows, and in every draw some expert is named by exactly 24 rows of some block.
All inputs are finite; a program needn't handle non-finite values. No bound on the sum of `accept_mask` on one device may be relied on, other than what follows from the above.
Results may differ from a plain program's by a relative error of at most 0.017.
Values may be sent and summed in bfloat16 or wider, within the bound.
A program may use at most 192 MiB of HBM per device.

v0:
```python
import jax
import jax.numpy as jnp
from jax import lax
from jax.sharding import PartitionSpec as P

DRAFT = 8
EXPERTS = 16
CAP = 24


def per_device(tokens, w_gate, w_up, w_down, router_logits, expert_ids, draft_lengths, accept_mask):
    tok_rows = tokens.shape[0]
    width = tokens.shape[1]
    top = expert_ids.shape[1]
    live = jnp.arange(DRAFT, dtype=jnp.int32)[None, :] < draft_lengths[:, None]
    live_rows = live.reshape(tok_rows)
    live_tokens = jnp.where(live_rows[:, None], tokens, jnp.zeros((), tokens.dtype))
    sig = jax.nn.sigmoid(router_logits)
    gates = 2.827 * sig / jnp.sum(sig, axis=1, keepdims=True)
    flat_ids = expert_ids.reshape(-1)
    onehot = (flat_ids[:, None] == jnp.arange(EXPERTS, dtype=jnp.int32)[None, :]).astype(jnp.int32)
    rank = jnp.cumsum(onehot, axis=0) - 1
    slot = jnp.sum(rank * onehot, axis=1)
    target = flat_ids * CAP + slot
    source = jnp.arange(tok_rows * top, dtype=jnp.int32) // top
    sendbuf = jnp.zeros((EXPERTS * CAP, width), tokens.dtype).at[target].set(live_tokens[source])
    received = lax.all_to_all(
        sendbuf.reshape(EXPERTS, CAP, width), "ep", split_axis=0, concat_axis=1, tiled=True
    )
    gate = jnp.einsum("emd,edf->emf", received, w_gate, preferred_element_type=jnp.float32)
    up = jnp.einsum("emd,edf->emf", received, w_up, preferred_element_type=jnp.float32)
    hidden = (jax.nn.silu(gate) * up).astype(jnp.bfloat16)
    partial_value = jnp.einsum("emf,efd->emd", hidden, w_down, preferred_element_type=jnp.float32)
    expert_out = lax.psum_scatter(
        partial_value.astype(jnp.bfloat16), "tp", scatter_dimension=2, tiled=True
    )
    returned = lax.all_to_all(expert_out, "ep", split_axis=1, concat_axis=0, tiled=True)
    flat_back = returned.reshape(EXPERTS * CAP, returned.shape[2])
    picked = flat_back[target].reshape(tok_rows, top, returned.shape[2])
    mixed = jnp.sum(gates[:, :, None] * picked.astype(jnp.float32), axis=1).astype(jnp.bfloat16)
    passed = accept_mask * live.astype(jnp.int32)
    prefix = jnp.cumprod(passed, axis=1)
    local_count = jnp.sum(prefix)
    total = lax.psum(local_count, "ep")
    accepted = total.reshape(1)
    return (mixed, accepted)


def solution(mesh):
    placed = (
        P(("groups", "ep"), None),
        P("ep", None, "tp"),
        P("ep", None, "tp"),
        P("ep", "tp", None),
        P(("groups", "ep"), None),
        P(("groups", "ep"), None),
        P(("groups", "ep")),
        P(("groups", "ep"), None),
    )
    return jax.shard_map(
        per_device,
        mesh=mesh,
        in_specs=placed,
        out_specs=(P(("groups", "ep"), "tp"), P("groups")),
        check_vma=False,
    )
```

profile of v0, /device:TPU:0, one launch (start us, length us, event | category | flops | bytes accessed | tf_op | source)
XLA Modules:
  0.0 279.7 jit_solution(1977247813884441354)
XLA Ops:
  7.2 0.0 reduce-scatter.2.cloned.1.call-start
  7.2 0.8 copy.21
  8.0 0.1 eq.29
  8.1 0.1 eq.25
  8.2 0.7 broadcast_multiply_fusion
  8.9 0.6 reduce-window.6
  9.5 0.2 slice_reduce_fusion
  9.7 0.1 copy.20
  9.8 0.1 mul.50
  9.9 0.7 iota_compare_fusion.2
  10.6 0.1 lt.45
  10.7 0.1 fusion.6
  10.8 1.1 broadcast_select_fusion
  11.9 19.2 %scatter_custom_fusion = bf16[384,7168]{1,0:T(8,128)(2,1)} fusion(s32[256]{0:T(256)S(1)} %bitcast.43, bf16[32,7168]{1,0:T(8,128)(2,1)S(1)} %broadcast_select_fusion, s32[1024]{0:T(1024)S(1)} %pad_clamp_fusion.1, bf16[]{:T(256)} %constant.38.clone.1), kind=kCustom, calls=%fused_computation.4 | custom fusion | bytes 5505026 | tf_op jit(solution)/shard_map/scatter | solution.py:26
  31.1 66.7 %all_to_all.33 = bf16[16,24,7168]{2,1,0:T(8,128)(2,1)S(1)} all-to-all(bf16[16,24,7168]{2,1,0:T(8,128)(2,1)} %bitcast.40), channel_id=1, replica_groups=mesh['groups'=2,'ep'=4,'tp'=4] {'ep'}, dimensions={0} | all-to-all | bytes 11010048 | tf_op jit(solution)/shard_map/all_to_all | solution.py:27
  97.9 0.5 copy.24
  98.3 0.0 copy-start
  98.3 2.4 copy-done
  100.7 11.8 %fusion.9 = f32[4,96,512]{2,1,0:T(8,128)S(1)} fusion(bf16[4,96,7168]{2,1,0:T(8,128)(2,1)S(1)} %bitcast.37, bf16[4,7168,512]{2,1,0:T(8,128)(2,1)} %param.9), kind=kOutput, calls=%fused_computation.34 | convolution fusion | flops 2818572288 | bytes 35651584 | tf_op jit(solution)/shard_map/emd,edf->emf/dot_general | solution.py:30
  112.5 15.7 %fusion.4 = bf16[4,96,512]{2,1,0:T(8,128)(2,1)S(1)} fusion(bf16[4,96,7168]{2,1,0:T(8,128)(2,1)} %bitcast.38, bf16[4,7168,512]{2,1,0:T(8,128)(2,1)} %param.10, f32[4,96,512]{2,1,0:T(8,128)S(1)} %fusion.9), kind=kOutput, calls=%fused_computation.10 | convolution fusion | flops 2819751936 | bytes 36044800 | tf_op jit(solution)/shard_map/emd,edf->emf/dot_general | solution.py:31
  128.3 16.5 %convolution_convert_fusion = bf16[4,96,7168]{2,1,0:T(8,128)(2,1)} fusion(bf16[4,96,512]{2,1,0:T(8,128)(2,1)S(1)} %fusion.4, bf16[4,512,7168]{2,1,0:T(8,128)(2,1)} %param.11), kind=kOutput, calls=%fused_computation.3 | convolution fusion | flops 2821324800 | bytes 35258368 | tf_op jit(solution)/shard_map/emf,efd->emd/dot_general | solution.py:33
  144.7 0.0 copy-start.2
  144.7 0.0 copy-start.3
  144.7 0.0 copy-start.1
  144.7 0.0 reduce-scatter.2.cloned.1.call-update
  144.8 99.3 %reduce-scatter.2.cloned.1.call-done = bf16[4,96,1792]{2,1,0:T(8,128)(2,1)} async-done(((bf16[4,96,7168]{2,1,0:T(8,128)(2,1)}), bf16[4,96,1792]{2,1,0:T(8,128)(2,1)}) %reduce-scatter.2.cloned.1.call-update) | async-done | bytes 1376272 | tf_op jit(solution)/shard_map/reduce_scatter | solution.py:34
  244.1 3.5 %copy.25 = bf16[4,96,1792]{2,0,1:T(4,128)(2,1)} copy(bf16[4,96,1792]{2,1,0:T(8,128)(2,1)} %reduce-scatter.2.cloned.1.call-done) | data formatting | bytes 2752512 | tf_op jit(solution)/shard_map/reduce_scatter | solution.py:34
  247.6 3.5 %all-to-all-start.1 = ((bf16[4,96,1792]{2,0,1:T(4,128)(2,1)}), bf16[4,96,1792]{2,0,1:T(4,128)(2,1)S(1)}, u32[]{:S(2)}, u32[]{:S(2)}) async-start(bf16[4,96,1792]{2,0,1:T(4,128)(2,1)} %copy.25), calls=%async_computation.2 | async-start | bytes 2752512 | tf_op jit(solution)/shard_map/all_to_all | solution.py:37
  251.1 0.0 copy-done.2
  251.1 0.0 copy-done.3
  251.2 0.1 broadcast_select_fusion.1
  251.2 0.2 reduce_window.9
  251.4 0.6 reduce_sum.42
  252.0 17.6 %psum.7 = s32[1]{0:T(128)} all-reduce(s32[1]{0:T(128)} %bitcast.12), channel_id=1, replica_groups=mesh['groups'=2,'ep'=4,'tp'=4] {'ep'}, use_global_device_ids=true, to_apply=%region_9.10 | all-reduce | flops 1 | bytes 8 | tf_op jit(solution)/shard_map/psum | solution.py:44
  269.6 0.0 copy-done.1
  269.7 0.1 copy.19
  269.8 0.0 all-to-all-done.1
  269.8 0.1 copy.26
  269.9 1.3 gather_fusion
  271.3 1.5 fusion.3
  (9 shorter events, 0.1 us)
Async XLA Ops:
  7.2 236.9 %reduce-scatter.2.cloned.1.call-start = ((), (), s32[]{:S(2)}) async-start(), calls=%async_computation.3 | async-start | bytes 6881280 | tf_op jit(solution)/shard_map/reduce_scatter | solution.py:34
  98.3 2.4 copy-start
  144.7 106.4 %copy-start.2 = (s32[4,8]{1,0:T(4,128)S(1)}, s32[4,8]{1,0:T(4,128)}, u32[]{:S(2)}) copy-start(s32[4,8]{1,0:T(4,128)} %param.15) | copy-start | bytes 388
  144.7 106.4 %copy-start.3 = (s32[4]{0:T(128)S(1)}, s32[4]{0:T(128)}, u32[]{:S(2)}) copy-start(s32[4]{0:T(128)} %param.14) | copy-start | bytes 52
  144.7 124.9 %copy-start.1 = (f32[32,8]{0,1:T(8,128)S(1)}, f32[32,8]{0,1:T(8,128)}, u32[]{:S(2)}) copy-start(f32[32,8]{0,1:T(8,128)} %param.12) | copy-start | bytes 3076
  247.6 22.2 %all-to-all-start.1 = ((bf16[4,96,1792]{2,0,1:T(4,128)(2,1)}), bf16[4,96,1792]{2,0,1:T(4,128)(2,1)S(1)}, u32[]{:S(2)}, u32[]{:S(2)}) async-start(bf16[4,96,1792]{2,0,1:T(4,128)(2,1)} %copy.25), calls=%async_computation.2 | async-start | bytes 2752512 | tf_op jit(solution)/shard_map/all_to_all | solution.py:37
Sparse Core Ops, SparseCore 0:
  144.9 99.1 reduce-scatter.1
where the time goes:
time: 280 us
  waiting for transfers between devices  99.3 us (35%)
  blocking collectives  84.3 us (30%)
  matrix products  44 us (16%)
  local copies, waits for them, and re-layouts  28.5 us (10%)
  between operations  14.1 us (5%)
  other arithmetic  5.75 us (2%)
  starting transfers between devices  3.58 us (1%)
    reduce_scatter x1, waiting for transfers between devices, per_device(): lax.psum_scatter(partial_value.astype(jnp.bfloat16), 'tp', scatter_dimens...  99.3 us
    all_to_all x1, blocking collectives, per_device(): lax.all_to_all(sendbuf.reshape(EXPERTS, CAP, width), 'ep', split_axis=0,...  66.7 us
    scatter x1, local copies, waits for them, and re-layouts, per_device(): jnp.zeros((EXPERTS * CAP, width), tokens.dtype).at[target]  19.2 us
    psum x1, blocking collectives, per_device(): total = lax.psum(local_count, 'ep')  17.6 us
    dot_general x1, matrix products, per_device(): jnp.einsum('emf,efd->emd', hidden, w_down, preferred_element_type=jnp.flo...  16.5 us
    dot_general x1, matrix products, per_device(): jnp.einsum('emd,edf->emf', received, w_up, preferred_element_type=jnp.flo...  15.7 us
    dot_general x1, matrix products, per_device(): jnp.einsum('emd,edf->emf', received, w_gate, preferred_element_type=jnp.f...  11.8 us
  transfers between devices with their start and end apart: 2, of which 1 were waited for; matrix products, arithmetic and copies ran while one was open for 0% of the time, Pallas kernels for 0%

commit v1 on v0

v1 whole, which is shorter than its diff:
```python
import jax
import jax.numpy as jnp
from jax import lax
from jax.sharding import PartitionSpec as P

DRAFT = 8
EXPERTS = 16


def per_device(tokens, w_gate, w_up, w_down, router_logits, expert_ids, draft_lengths, accept_mask):
    tok_rows = tokens.shape[0]
    local = w_gate.shape[0]
    me = lax.axis_index("ep")
    live = jnp.arange(DRAFT, dtype=jnp.int32)[None, :] < draft_lengths[:, None]
    sig = jax.nn.sigmoid(router_logits)
    gates = 2.827 * sig / jnp.sum(sig, axis=1, keepdims=True)
    named = expert_ids[:, :, None] == jnp.arange(EXPERTS, dtype=jnp.int32)[None, None, :]
    dense = jnp.sum(jnp.where(named, gates[:, :, None], 0.0), axis=1)
    dense = jnp.where(live.reshape(tok_rows)[:, None], dense, 0.0)
    rows = lax.all_gather(tokens, "ep", axis=0, tiled=True)
    dense = lax.all_gather(dense, "ep", axis=0, tiled=True)
    mine = lax.dynamic_slice_in_dim(dense, me * local, local, axis=1)
    gate = jnp.einsum("md,edf->emf", rows, w_gate, preferred_element_type=jnp.float32)
    up = jnp.einsum("md,edf->emf", rows, w_up, preferred_element_type=jnp.float32)
    hidden = (jax.nn.silu(gate) * up * mine.T[:, :, None]).astype(jnp.bfloat16)
    partial = jnp.einsum("emf,efd->md", hidden, w_down, preferred_element_type=jnp.float32)
    partial = partial.astype(jnp.bfloat16)
    partial = lax.psum_scatter(partial, "ep", scatter_dimension=0, tiled=True)
    mixed = lax.psum_scatter(partial, "tp", scatter_dimension=1, tiled=True)
    passed = accept_mask * live.astype(jnp.int32)
    accepted = lax.psum(jnp.sum(jnp.cumprod(passed, axis=1)), "ep").reshape(1)
    return (mixed, accepted)


def solution(mesh):
    placed = (
        P(("groups", "ep"), None),
        P("ep", None, "tp"),
        P("ep", None, "tp"),
        P("ep", "tp", None),
        P(("groups", "ep"), None),
        P(("groups", "ep"), None),
        P(("groups", "ep")),
        P(("groups", "ep"), None),
    )
    return jax.shard_map(
        per_device,
        mesh=mesh,
        in_specs=placed,
        out_specs=(P(("groups", "ep"), "tp"), P("groups")),
        check_vma=False,
    )
```

time: 280 us -> 141 us (0.50)
  blocking collectives: 84.3 us -> 11.1 us
  waiting for transfers between devices: 99.3 us -> 65 us
  local copies, waits for them, and re-layouts: 28.5 us -> 0.21 us
  starting transfers between devices: 3.58 us -> 0.12 us
    all_to_all x1 -> x0, blocking collectives: 66.7 us -> none  [per_device(): lax.all_to_all(sendbuf.reshape(EXPERTS, CAP, width), 'ep', split_axis=0,...]
    reduce_scatter x1 -> x2, waiting for transfers between devices: 99.3 us -> 48.1 us  [the longest x1 29.7 us: per_device(): partial = lax.psum_scatter(partial, 'ep', scatter_dimension=0, tiled=True)]
    scatter x1 -> x0, local copies, waits for them, and re-layouts: 19.2 us -> none  [per_device(): jnp.zeros((EXPERTS * CAP, width), tokens.dtype).at[target]]
    all_gather x0 -> x1, waiting for transfers between devices: none -> 16.2 us  [per_device(): rows = lax.all_gather(tokens, 'ep', axis=0, tiled=True)]
    psum x1, blocking collectives: 17.6 us -> 4.89 us  [per_device(): accepted = lax.psum(jnp.sum(jnp.cumprod(passed, axis=1)), 'ep').reshape(1)]
    all_gather x0 -> x1, blocking collectives: none -> 6.21 us  [per_device(): dense = lax.all_gather(dense, 'ep', axis=0, tiled=True)]
    all_to_all x1 -> x0, starting transfers between devices: 3.54 us -> none  [per_device(): lax.all_to_all(expert_out, 'ep', split_axis=1, concat_axis=0, tiled=True)]
    reduce_scatter x1 -> x0, local copies, waits for them, and re-layouts: 3.48 us -> none  [per_device(): lax.psum_scatter(partial_value.astype(jnp.bfloat16), 'tp', scatter_dimens...]
  transfers between devices with their start and end apart: 2 -> 3, of which waited for: 1 -> 3; matrix products, arithmetic and copies ran while one was open for 0% -> 3% of each run, Pallas kernels for 0% -> 0%
where the time goes in v1:
time: 141 us
  waiting for transfers between devices  65 us (46%)
  matrix products  46.6 us (33%)
  between operations  13.8 us (10%)
  blocking collectives  11.1 us (8%)
  other arithmetic  3.75 us (3%)
    reduce_scatter x1, waiting for transfers between devices, per_device(): partial = lax.psum_scatter(partial, 'ep', scatter_dimension=0, tiled=True)  29.7 us
    reduce_scatter x1, waiting for transfers between devices, per_device(): mixed = lax.psum_scatter(partial, 'tp', scatter_dimension=1, tiled=True)  18.4 us
    dot_general x1, matrix products, per_device(): jnp.einsum('md,edf->emf', rows, w_gate, preferred_element_type=jnp.float32)  17.8 us
    all_gather x1, waiting for transfers between devices, per_device(): rows = lax.all_gather(tokens, 'ep', axis=0, tiled=True)  16.2 us
    dot_general x1, matrix products, per_device(): jnp.einsum('emf,efd->md', hidden, w_down, preferred_element_type=jnp.floa...  14.8 us
    dot_general x1, matrix products, per_device(): jnp.einsum('md,edf->emf', rows, w_up, preferred_element_type=jnp.float32)  14 us
    all_gather x1, blocking collectives, per_device(): dense = lax.all_gather(dense, 'ep', axis=0, tiled=True)  6.21 us
    psum x1, blocking collectives, per_device(): accepted = lax.psum(jnp.sum(jnp.cumprod(passed, axis=1)), 'ep').reshape(1)  4.89 us
  transfers between devices with their start and end apart: 3, of which 3 were waited for; matrix products, arithmetic and copies ran while one was open for 3% of the time, Pallas kernels for 0%

profile of v1, /device:TPU:0, one launch (start us, length us, event | category | flops | bytes accessed | tf_op | source)
XLA Modules:
  0.0 140.5 jit_solution(3762252298330406964)
XLA Ops:
  7.2 0.0 all-gather.3.cloned.1.call-start
  7.2 0.7 all-gather.3.cloned.1.call-update
  7.9 0.0 reduce-scatter.3.cloned.1.call-start
  7.9 0.7 iota_compare_fusion.1
  8.7 0.1 lt.26
  8.8 0.7 fusion.20
  9.5 0.7 multiply_divide_fusion
  10.2 0.7 select_reduce_fusion
  10.9 6.2 %all-gather = f32[4,32,16]{1,2,0:T(8,128)S(1)} all-gather(f32[1,32,16]{1,2,0:T(8,128)S(1)} %select_bitcast_fusion), channel_id=1, replica_groups=mesh['groups'=2,'ep'=4,'tp'=4] {'ep'}, dimensions={0}, use_global_device_ids=true | all-gather | bytes 10240 | tf_op jit(solution)/shard_map/all_gather | solution.py:21
  17.1 0.1 reshape.28
  17.2 16.2 %all-gather.3.cloned.1.call-done = bf16[128,7168]{1,0:T(8,128)(2,1)} async-done(((bf16[32,7168]{1,0:T(8,128)(2,1)}), bf16[128,7168]{1,0:T(8,128)(2,1)}) %all-gather.3.cloned.1.call-update) | async-done | bytes 1835024 | tf_op jit(solution)/shard_map/all_gather | solution.py:20
  33.4 0.0 copy-start.2
  33.4 17.8 %fusion.5 = f32[4,128,512]{1,2,0:T(8,128)S(1)} fusion(bf16[4,7168,512]{2,1,0:T(8,128)(2,1)} %param.9, bf16[128,7168]{1,0:T(8,128)(2,1)} %all-gather.3.cloned.1.call-done), kind=kOutput, calls=%fused_computation.6 | convolution fusion | flops 3758096384 | bytes 32243712 | tf_op jit(solution)/shard_map/md,edf->emf/dot_general | solution.py:23
  51.2 0.0 copy-done.2
  51.2 0.0 copy-start
  51.2 0.0 copy-start.1
  51.2 14.0 %fusion.17 = bf16[4,128,512]{1,2,0:T(8,128)(2,1)S(1)} fusion(bf16[4,7168,512]{2,1,0:T(8,128)(2,1)} %param.10, bf16[128,7168]{1,0:T(8,128)(2,1)S(1)} %copy-done.2, f32[4,128,512]{1,2,0:T(8,128)S(1)} %fusion.5, f32[4,128]{1,0:T(4,128)S(1)} %dynamic-slice_bitcast_fusion), kind=kOutput, calls=%fused_computation.10 | convolution fusion | flops 3759931392 | bytes 32770048 | tf_op jit(solution)/shard_map/md,edf->emf/dot_general | solution.py:24
  65.2 14.8 %fusion = bf16[128,7168]{1,0:T(8,128)(2,1)} fusion(bf16[4,128,512]{1,2,0:T(8,128)(2,1)S(1)} %fusion.17, bf16[4,512,7168]{2,1,0:T(8,128)(2,1)} %param.11), kind=kOutput, calls=%fused_computation.1 | convolution fusion | flops 3759013888 | bytes 31719424 | tf_op jit(solution)/shard_map/emf,efd->md/dot_general | solution.py:26
  80.0 0.0 reduce-scatter.3.cloned.1.call-update
  80.0 0.0 reduce-scatter.5.cloned.1.call-start
  80.1 29.7 %reduce-scatter.3.cloned.1.call-done = bf16[32,7168]{1,0:T(8,128)(2,1)} async-done(((bf16[128,7168]{1,0:T(8,128)(2,1)}), bf16[32,7168]{1,0:T(8,128)(2,1)}) %reduce-scatter.3.cloned.1.call-update) | async-done | bytes 458768 | tf_op jit(solution)/shard_map/reduce_scatter | solution.py:28
  109.8 0.0 reduce-scatter.5.cloned.1.call-update
  109.8 0.0 copy-done
  109.8 0.0 copy-done.1
  109.8 0.1 broadcast_select_fusion
  109.9 0.2 reduce_window.9
  110.1 0.6 reduce_sum.29
  110.7 4.9 %psum.7 = s32[1]{0:T(128)} all-reduce(s32[1]{0:T(128)} %bitcast.6), channel_id=1, replica_groups=mesh['groups'=2,'ep'=4,'tp'=4] {'ep'}, use_global_device_ids=true, to_apply=%region_6.7 | all-reduce | flops 1 | bytes 8 | tf_op jit(solution)/shard_map/psum | solution.py:31
  115.6 18.4 %reduce-scatter.5.cloned.1.call-done = bf16[32,1792]{1,0:T(8,128)(2,1)} async-done(((bf16[32,7168]{1,0:T(8,128)(2,1)}), bf16[32,1792]{1,0:T(8,128)(2,1)}) %reduce-scatter.5.cloned.1.call-update) | async-done | bytes 114704 | tf_op jit(solution)/shard_map/reduce_scatter | solution.py:29
  (3 shorter events, 0.0 us)
Async XLA Ops:
  7.2 26.2 %all-gather.3.cloned.1.call-start = ((), (), s32[]{:S(2)}) async-start(), calls=%async_computation.2 | async-start | bytes 2293760 | tf_op jit(solution)/shard_map/all_gather | solution.py:20
  7.9 101.9 %reduce-scatter.3.cloned.1.call-start = ((), (), s32[]{:S(2)}) async-start(), calls=%async_computation.3 | async-start | bytes 2293760 | tf_op jit(solution)/shard_map/reduce_scatter | solution.py:28
  33.4 17.8 %copy-start.2 = (bf16[128,7168]{1,0:T(8,128)(2,1)S(1)}, bf16[128,7168]{1,0:T(8,128)(2,1)}, u32[]{:S(2)}) copy-start(bf16[128,7168]{1,0:T(8,128)(2,1)} %all-gather.3.cloned.1.call-done) | copy-start | bytes 5505028
  51.2 58.6 %copy-start = (s32[4,8]{1,0:T(4,128)S(1)}, s32[4,8]{1,0:T(4,128)}, u32[]{:S(2)}) copy-start(s32[4,8]{1,0:T(4,128)} %param.15) | copy-start | bytes 388
  51.2 58.6 %copy-start.1 = (s32[4]{0:T(128)S(1)}, s32[4]{0:T(128)}, u32[]{:S(2)}) copy-start(s32[4]{0:T(128)} %param.14) | copy-start | bytes 52
  80.0 54.0 %reduce-scatter.5.cloned.1.call-start = ((), (), s32[]{:S(2)}) async-start(), calls=%async_computation.4 | async-start | bytes 573440 | tf_op jit(solution)/shard_map/reduce_scatter | solution.py:29
Sparse Core Ops, SparseCore 0:
  9.5 23.8 all-gather.2
  80.2 29.5 reduce-scatter.2
  112.6 21.3 reduce-scatter.4

commit v2 on v1

v2 whole, which is shorter than its diff:
```python
import functools

import jax
import jax.numpy as jnp
from jax import lax
from jax.experimental import pallas as pl
from jax.experimental.pallas import tpu as pltpu
from jax.sharding import PartitionSpec as P

DRAFT = 8
EXPERTS = 16
LANES = 128
MESH = pl.DeviceIdType.MESH


def kernel(n_ep, n_tp, pieces, slots, lens, tokens, logits, ids, mask, wg, wu, wd,
           out, count, xbuf, gbuf, wgb, wub, wdb, accg, accu, hid, pbuf, r1, s1, r2, s2, r3, own,
           gsem, usem, dsem, xr, xs, ps, fs, s1s, s1r, s2s, s2r, s3s, s3r):
    me, tp = lax.axis_index("ep"), lax.axis_index("tp")
    chip, core = me // 2, me % 2
    n_chip = n_ep // 2
    partner = me + 1 - 2 * core
    rows, width = tokens.shape
    local, _, ff = wg.shape
    kc = width // pieces
    cols = width // n_tp
    total_rows = n_ep * rows
    steps = pieces * local

    def gu(s, slot):
        e, at = s % local, pl.multiple_of((s // local) * kc, kc)
        return (pltpu.make_async_copy(wg.at[e, pl.ds(at, kc), :], wgb.at[slot], gsem.at[slot]),
                pltpu.make_async_copy(wu.at[e, pl.ds(at, kc), :], wub.at[slot], usem.at[slot]))

    def down(j):
        z = lax.rem(tp + 1 + j, n_tp)
        return pltpu.make_async_copy(wd.at[:, :, pl.ds(pl.multiple_of(z * cols, cols), cols)], wdb.at[j], dsem.at[j])

    for s in range(slots):
        for c in gu(s, s):
            c.start()

    sig = 1.0 / (1.0 + jnp.exp(-logits[...]))
    gates = 2.827 * sig / jnp.sum(sig, axis=1, keepdims=True)
    lane = lax.broadcasted_iota(jnp.int32, (rows, LANES), 1)
    row = lax.broadcasted_iota(jnp.int32, (rows, LANES), 0)
    dense = jnp.zeros((rows, LANES), jnp.float32)
    named = ids[...]
    for k in range(logits.shape[1]):
        dense = dense + jnp.where(named[:, k:k + 1] == lane, gates[:, k:k + 1], 0.0)
    requests = mask.shape[0]
    end = jnp.zeros((rows, LANES), jnp.int32)
    short = jnp.zeros((requests, DRAFT), jnp.int32)
    request = lax.broadcasted_iota(jnp.int32, (requests, DRAFT), 0)
    draft = lax.broadcasted_iota(jnp.int32, (requests, DRAFT), 1)
    for r in range(requests):
        end = jnp.where(row >= r * DRAFT, r * DRAFT + lens[r], end)
        short = jnp.where(request == r, lens[r], short)
    dense = jnp.where(row < end, dense, 0.0)
    passed = jnp.where(draft < short, mask[...], 0).astype(jnp.float32)
    run = passed[:, 0:1]
    kept = run
    for j in range(1, DRAFT):
        run = run * passed[:, j:j + 1]
        kept = kept + run
    gbuf[me] = jnp.where(lane == EXPERTS, jnp.sum(kept), dense)
    xbuf[me] = tokens[...]

    peers = [lax.rem(chip + d, n_chip) * 2 + core for d in range(1, n_chip)]
    sources = [lax.rem(chip + n_chip - d, n_chip) * 2 + core for d in range(1, n_chip)]
    barrier = pltpu.get_barrier_semaphore()
    for peer in peers + [partner]:
        pl.semaphore_signal(barrier, inc=1, device_id={"ep": peer}, device_id_type=MESH)
    for d in range(1, n_tp):
        pl.semaphore_signal(barrier, inc=1, device_id={"tp": lax.rem(tp + d, n_tp)}, device_id_type=MESH)
    pl.semaphore_wait(barrier, n_chip + n_tp - 1)

    def view(source, p):
        if p == pieces:
            return gbuf.at[source]
        return xbuf.at[source, :, pl.ds(p * kc, kc)]

    def move(source, p, send, target):
        src = view(source, p)
        if p < pieces and source is me:
            src = tokens.at[:, pl.ds(p * kc, kc)]
        return pltpu.make_async_remote_copy(src_ref=src, dst_ref=view(source, p), send_sem=send,
                                            recv_sem=xr.at[source, p], device_id={"ep": target}, device_id_type=MESH)

    sends = []
    order = [0, pieces] + list(range(1, pieces))
    for p in order:
        for d, peer in enumerate(peers):
            sends.append(move(me, p, xs.at[d, p], peer))
            sends[-1].start()
        sends.append(move(me, p, ps.at[p], partner))
        sends[-1].start()

    def forward(p):
        for d, source in enumerate(sources):
            move(source, p, xs.at[d, p], partner).wait_recv()
            sends.append(move(source, p, fs.at[d, p], partner))
            sends[-1].start()

    def landed(p):
        move(partner, p, ps.at[p], partner).wait_recv()
        for source in sources:
            move(source + 1 - 2 * core, p, ps.at[p], partner).wait_recv()

    forward(0)
    forward(pieces)
    for p in range(pieces):
        if p + 1 < pieces:
            forward(p + 1)
        for j in range(n_tp):
            if max(0, pieces - n_tp + j) == p:
                down(j).start()
        landed(p)

        @pl.loop(0, local)
        def _(e):
            s = p * local + e
            slot = lax.rem(s, slots)
            for c in gu(s, slot):
                c.wait()
            x = xbuf[:, :, p * kc:(p + 1) * kc].reshape(total_rows, kc)
            g = jnp.dot(x, wgb[slot], preferred_element_type=jnp.float32)
            u = jnp.dot(x, wub[slot], preferred_element_type=jnp.float32)
            if p == 0:
                accg[e] = g
                accu[e] = u
            else:
                accg[e] += g
                accu[e] += u
            if (p + 1) * local - 1 + slots < steps or p * local + slots < steps:
                @pl.when(s + slots < steps)
                def _():
                    for c in gu(s + slots, slot):
                        c.start()
    landed(pieces)

    dense = gbuf[...].reshape(total_rows, LANES)
    lane = lax.broadcasted_iota(jnp.int32, (total_rows, LANES), 1)
    for e in range(local):
        gate = jnp.sum(jnp.where(lane == me * local + e, dense, 0.0), axis=1, keepdims=True)
        v = accg[e]
        hid[:, e * ff:(e + 1) * ff] = (v / (1.0 + jnp.exp(-v)) * accu[e] * gate).astype(jnp.bfloat16)

    def first(j):
        return pltpu.make_async_remote_copy(
            src_ref=pbuf.at[j, :, 1 - core], dst_ref=r1.at[j], send_sem=s1s.at[j], recv_sem=s1r.at[j],
            device_id={"ep": partner}, device_id_type=MESH)

    def second(j, d):
        to = lax.rem(chip + d, n_chip)
        return pltpu.make_async_remote_copy(
            src_ref=s1.at[j, to], dst_ref=r2.at[j, d - 1], send_sem=s2s.at[j, d - 1], recv_sem=s2r.at[j, d - 1],
            device_id={"ep": to * 2 + core}, device_id_type=MESH)

    def third(j):
        return pltpu.make_async_remote_copy(
            src_ref=s2.at[j], dst_ref=r3.at[j], send_sem=s3s.at[j], recv_sem=s3r.at[j],
            device_id={"tp": lax.rem(tp + 1 + j, n_tp)}, device_id_type=MESH)

    def stage2(j):
        first(j).wait_recv()
        s1[j] = (pbuf[j, :, core].astype(jnp.float32) + r1[j].astype(jnp.float32)).astype(jnp.bfloat16)
        for d in range(1, n_chip):
            second(j, d).start()

    def stage3(j):
        value = s1[j, chip].astype(jnp.float32)
        for d in range(1, n_chip):
            second(j, d).wait_recv()
            value = value + r2[j, d - 1].astype(jnp.float32)
        if j < n_tp - 1:
            s2[j] = value.astype(jnp.bfloat16)
            third(j).start()
        else:
            own[...] = value

    for j in range(n_tp):
        down(j).wait()
        y = jnp.dot(hid[...], wdb[j].reshape(local * ff, cols), preferred_element_type=jnp.float32)
        pbuf[j] = y.astype(jnp.bfloat16).reshape(n_chip, 2, rows, cols)
        first(j).start()
        if j >= 2:
            stage3(j - 2)
        if j >= 1:
            stage2(j - 1)
    if n_tp >= 2:
        stage3(n_tp - 2)
    stage2(n_tp - 1)
    stage3(n_tp - 1)

    rowid = lax.broadcasted_iota(jnp.int32, (rows, LANES), 0)
    lane = lax.broadcasted_iota(jnp.int32, (rows, LANES), 1)
    tally = jnp.zeros((rows, LANES), jnp.float32)
    for i in range(n_ep):
        tally = tally + gbuf[i]
    count[0] = jnp.sum(jnp.where((rowid == 0) & (lane == EXPERTS), tally, 0.0)).astype(jnp.int32)

    value = own[...]
    for j in range(n_tp - 1):
        third(j).wait_recv()
        value = value + r3[j].astype(jnp.float32)
    out[...] = value.astype(jnp.bfloat16)

    for c in sends:
        c.wait_send()
    for j in range(n_tp):
        first(j).wait_send()
        for d in range(1, n_chip):
            second(j, d).wait_send()
        if j < n_tp - 1:
            third(j).wait_send()


def per_device(n_ep, n_tp, tokens, w_gate, w_up, w_down, router_logits, expert_ids, draft_lengths, accept_mask):
    rows, width = tokens.shape
    local, _, ff = w_gate.shape
    n_chip = n_ep // 2
    pieces = 7 if width % (7 * LANES) == 0 else 1
    kc, cols = width // pieces, width // n_tp
    slots = min(8, pieces * local)
    vmem, hbm, smem = [pl.BlockSpec(memory_space=m) for m in (pltpu.VMEM, pl.ANY, pltpu.SMEM)]
    bf, f32, dma = jnp.bfloat16, jnp.float32, pltpu.SemaphoreType.DMA
    back = max(1, n_chip - 1)
    return pl.pallas_call(
        functools.partial(kernel, n_ep, n_tp, pieces, slots),
        out_shape=(jax.ShapeDtypeStruct((rows, cols), bf), jax.ShapeDtypeStruct((1,), jnp.int32)),
        in_specs=[smem, vmem, vmem, vmem, vmem, hbm, hbm, hbm],
        out_specs=(vmem, smem),
        scratch_shapes=[
            pltpu.VMEM((n_ep, rows, width), bf),
            pltpu.VMEM((n_ep, rows, LANES), f32),
            pltpu.VMEM((slots, kc, ff), bf),
            pltpu.VMEM((slots, kc, ff), bf),
            pltpu.VMEM((n_tp, local, ff, cols), bf),
            pltpu.VMEM((local, n_ep * rows, ff), f32),
            pltpu.VMEM((local, n_ep * rows, ff), f32),
            pltpu.VMEM((n_ep * rows, local * ff), bf),
            pltpu.VMEM((n_tp, n_chip, 2, rows, cols), bf),
            pltpu.VMEM((n_tp, n_chip, rows, cols), bf),
            pltpu.VMEM((n_tp, n_chip, rows, cols), bf),
            pltpu.VMEM((n_tp, back, rows, cols), bf),
            pltpu.VMEM((n_tp, rows, cols), bf),
            pltpu.VMEM((n_tp, rows, cols), bf),
            pltpu.VMEM((rows, cols), f32),
            dma((slots,)), dma((slots,)), dma((n_tp,)),
            dma((n_ep, pieces + 1)), dma((back, pieces + 1)), dma((pieces + 1,)), dma((back, pieces + 1)),
            dma((n_tp,)), dma((n_tp,)), dma((n_tp, back)), dma((n_tp, back)), dma((n_tp,)), dma((n_tp,)),
        ],
        compiler_params=pltpu.CompilerParams(
            collective_id=0, has_side_effects=True, vmem_limit_bytes=66_000_000),
    )(draft_lengths, tokens, router_logits, expert_ids, accept_mask, w_gate, w_up, w_down)


def solution(mesh):
    placed = (
        P(("groups", "ep"), None),
        P("ep", None, "tp"),
        P("ep", None, "tp"),
        P("ep", "tp", None),
        P(("groups", "ep"), None),
        P(("groups", "ep"), None),
        P(("groups", "ep")),
        P(("groups", "ep"), None),
    )
    return jax.shard_map(
        functools.partial(per_device, mesh.shape["ep"], mesh.shape["tp"]),
        mesh=mesh,
        in_specs=placed,
        out_specs=(P(("groups", "ep"), "tp"), P("groups")),
        check_vma=False,
    )
```

time: 141 us -> 59 us (0.42)
  waiting for transfers between devices: 65 us -> 0 us
  Pallas kernels: 0 us -> 52 us
  matrix products: 46.6 us -> 0 us
  between operations: 13.8 us -> 2.45 us
  blocking collectives: 11.1 us -> 0 us
  local copies, waits for them, and re-layouts: 0.21 us -> 4.27 us
  other arithmetic: 3.75 us -> 0 us
    pallas_call x0 -> x1, Pallas kernels: none -> 52 us  [per_device(): pl.pallas_call(functools.partial(kernel, n_ep, n_tp, pieces, slots), out_...]
    reduce_scatter x2 -> x0, waiting for transfers between devices: 48.1 us -> none  [the longest x1 29.7 us: per_device(): partial = lax.psum_scatter(partial, 'ep', scatter_dimension=0, tiled=True)]
    dot_general x3 -> x0, matrix products: 46.6 us -> none  [the longest x1 17.8 us: per_device(): jnp.einsum('md,edf->emf', rows, w_gate, preferred_element_type=jnp.float32)]
    all_gather x1 -> x0, waiting for transfers between devices: 16.2 us -> none  [per_device(): rows = lax.all_gather(tokens, 'ep', axis=0, tiled=True)]
    all_gather x1 -> x0, blocking collectives: 6.21 us -> none  [per_device(): dense = lax.all_gather(dense, 'ep', axis=0, tiled=True)]
    psum x1 -> x0, blocking collectives: 4.89 us -> none  [per_device(): accepted = lax.psum(jnp.sum(jnp.cumprod(passed, axis=1)), 'ep').reshape(1)]
    unnamed x7 -> x3, local copies, waits for them, and re-layouts: 0.1 us -> 4.27 us
    reduce_sum x3 -> x0, other arithmetic: 2.06 us -> none  [the longest x1 0.71 us: per_device(): dense = jnp.sum(jnp.where(named, gates[:, :, None], 0.0), axis=1)]
  transfers between devices with their start and end apart: 3 -> 0, of which waited for: 3 -> 0; matrix products, arithmetic and copies ran while one was open for 3% -> 0% of each run, Pallas kernels for 0% -> 0%
where the time goes in v2:
time: 59 us; the launch traced here: 58.8 us
  Pallas kernels  52 us (88%)
  local copies, waits for them, and re-layouts  4.27 us (7%)
  between operations  2.45 us (4%)
    pallas_call x1, Pallas kernels, per_device(): pl.pallas_call(functools.partial(kernel, n_ep, n_tp, pieces, slots), out_...  52 us
    unnamed x3, local copies, waits for them, and re-layouts  4.27 us

profile of v2, /device:TPU:0, one launch (start us, length us, event | category | flops | bytes accessed | tf_op | source)
XLA Modules:
  0.0 58.8 jit_solution(16307735787880281819)
XLA Ops:
  0.6 1.4 %copy.10.logits = f32[32,8]{1,0:T(8,128)} copy(f32[32,8]{0,1:T(8,128)} %param.12) | data formatting | bytes 2048 | tf_op args[4]
  2.0 1.4 %copy.11.ids = s32[32,8]{1,0:T(8,128)} copy(s32[32,8]{0,1:T(8,128)} %param.13) | data formatting | bytes 2048 | tf_op args[5]
  3.4 52.0 %shard_map.95 = (bf16[32,1792]{1,0:T(8,128)(2,1)}, s32[1]{0:T(128)}) custom-call(s32[4]{0:T(128)} %lens.1, bf16[32,7168]{1,0:T(8,128)(2,1)} %tokens.1, f32[32,8]{1,0:T(8,128)} %copy.10.logits, s32[32,8]{1,0:T(8,128)} %copy.11.ids, s32[4,8]{1,0:T(4,128)} %mask.1, bf16[4,7168,512]{2,1,0:T(8,128)(2,1)} %wg.1, bf16[4,7168,512]{2,1,0:T(8,128)(2,1)} %wu.1, ...), custom_call_target="tpu_custom_call" | custom-call | tf_op jit(solution)/shard_map/pallas_call | solution.py:229
  55.4 1.6 %copy.14 = bf16[32,1792]{1,0:T(8,128)(2,1)} copy(bf16[32,1792]{1,0:T(8,128)(2,1)} %get-tuple-element.4) | data formatting | bytes 229376
